TPU v7x, 32 devices: a whole 2x2x4 slice. The times are simulated.
32 devices in a mesh: groups: 2 (over x), expert: 16 (over z, y, core).
Axes of the slice: x: 2, y: 2, z: 4, core: 2. Of those that a mesh axis runs over, the one named last changes fastest.
Arguments:
- tokens: bfloat16 [512, 6144], P(('groups', 'expert')), parts along dimension 0, may hold values from -6 to 6
- route_ids: int32 [512, 2], P(('groups', 'expert')), parts along dimension 0, may hold values from 0 to 7, all different within a row; in each aligned block of 16 rows (0 to 15, 16 to 31, ...) at most 6 rows name the same one
- route_logits: float32 [512, 2], P(('groups', 'expert')), parts along dimension 0, may hold values from -6 to 6
- old_place: int32 [16], replicated, may hold values from 0 to 15, each once
- new_place: int32 [16], replicated, may hold values from 0 to 15, each once
- held_gate: bfloat16 [32, 6144, 128], P(('groups', 'expert')), parts along dimension 0, may hold values from -0.078125 to 0.078125
- held_up: bfloat16 [32, 6144, 128], P(('groups', 'expert')), parts along dimension 0, may hold values from -0.078125 to 0.078125
- held_down: bfloat16 [32, 6144, 128], P(('groups', 'expert')), parts along dimension 0, may hold values from -0.375 to 0.375
Outputs:
- moe_output: bfloat16 [512, 6144], P(('groups', 'expert')), parts along dimension 0
- moved_gate: bfloat16 [32, 6144, 128], P(('groups', 'expert')), parts along dimension 0
- moved_up: bfloat16 [32, 6144, 128], P(('groups', 'expert')), parts along dimension 0
- moved_down: bfloat16 [32, 6144, 128], P(('groups', 'expert')), parts along dimension 0
There are 2 independent parts, one for each index of `groups`. A program takes and returns all parts, laid end to end along the dimension named above; an argument that names none is the same for every part. Nothing has to cross between parts.
Inputs may be any that keep to these rules, and one draw needn't show every extreme that they name: `route_ids`: within the rows of one device (aligned blocks of 16 rows) no expert is named by more than 6 rows, a bound that some block reaches; the two ids of a row differ. `old_place`: each device appears once. `new_place`: each device appears once.
All inputs are finite; a program needn't handle non-finite values.
Results may differ from a plain program's by a relative error of at most 0.0058.
Values may be sent and summed in bfloat16 or wider, within the bound.
A program may use at most 128 MiB of HBM per device.

v0:
```python
import jax
import jax.numpy as jnp
from jax import lax
from jax.sharding import PartitionSpec as P

EXPERTS = 8
CAP = 6


def inverse_of(placement, device_ids):
    return jnp.sum(
        jnp.where(placement[:, None] == device_ids[None, :], device_ids[:, None], 0), axis=0
    )


def per_device(
    tokens, route_ids, route_logits, old_place, new_place, held_gate, held_up, held_down
):
    devices = lax.axis_size("expert")
    width = tokens.shape[1]
    tok_rows = tokens.shape[0]
    device_ids = jnp.arange(devices, dtype=jnp.int32)
    slot_new_at = inverse_of(new_place, device_ids)
    slot_old_at = inverse_of(old_place, device_ids)
    source_of = jnp.take(old_place, slot_new_at)
    pieces = (
        lax.all_to_all(held_gate, "expert", split_axis=1, concat_axis=0, tiled=True),
        lax.all_to_all(held_up, "expert", split_axis=1, concat_axis=0, tiled=True),
        lax.all_to_all(held_down, "expert", split_axis=1, concat_axis=0, tiled=True),
    )
    reordered = (
        jnp.take(pieces[0], source_of, axis=0),
        jnp.take(pieces[1], source_of, axis=0),
        jnp.take(pieces[2], source_of, axis=0),
    )
    migrated = (
        lax.all_to_all(reordered[0], "expert", split_axis=0, concat_axis=1, tiled=True),
        lax.all_to_all(reordered[1], "expert", split_axis=0, concat_axis=1, tiled=True),
        lax.all_to_all(reordered[2], "expert", split_axis=0, concat_axis=1, tiled=True),
    )
    w_gate, w_up, w_down = (held_gate, held_up, held_down)
    blocks = devices // EXPERTS
    expert_at = slot_old_at // blocks
    expert_ids = jnp.arange(EXPERTS, dtype=jnp.int32)
    route_hits = route_ids[:, :, None] == expert_ids[None, None, :]
    routed = jnp.any(route_hits, axis=1).astype(jnp.int32)
    position = jnp.cumsum(routed, axis=0) - 1
    bucket_ids = jnp.arange(CAP, dtype=jnp.int32)
    bucket_table = (routed[:, :, None] == 1) & (position[:, :, None] == bucket_ids[None, None, :])
    picker = bucket_table.reshape(tok_rows, EXPERTS * CAP).astype(jnp.bfloat16)
    buckets = lax.dot_general(
        picker, tokens, (((0,), (0,)), ((), ())), preferred_element_type=jnp.float32
    )
    buckets = buckets.astype(jnp.bfloat16).reshape(EXPERTS, CAP, width)
    outgoing = jnp.take(buckets, expert_at, axis=0)
    incoming = lax.all_to_all(outgoing, "expert", split_axis=0, concat_axis=0, tiled=True)
    sources = incoming.shape[0]
    count = incoming.shape[1]
    stacked = incoming.reshape(sources * count, width)
    gate_value = jnp.dot(stacked, w_gate[0], preferred_element_type=jnp.float32)
    up_value = jnp.dot(stacked, w_up[0], preferred_element_type=jnp.float32)
    hidden = (jax.nn.silu(gate_value) * up_value).astype(jnp.bfloat16)
    partial_value = lax.dot_general(
        hidden, w_down[0], (((1,), (1,)), ((), ())), preferred_element_type=jnp.float32
    )
    partial_value = partial_value.astype(jnp.bfloat16).reshape(sources, count, width)
    returned = lax.all_to_all(partial_value, "expert", split_axis=0, concat_axis=0, tiled=True)
    membership = (expert_at[None, :] == expert_ids[:, None]).astype(jnp.bfloat16)
    expert_sum = jnp.dot(
        membership, returned.reshape(devices, CAP * width), preferred_element_type=jnp.float32
    )
    expert_sum = expert_sum.reshape(EXPERTS * CAP, width)
    token_slot = jnp.take_along_axis(position, route_ids, axis=1)
    row_index = route_ids * CAP + token_slot
    selected = jnp.take(expert_sum, row_index.reshape(-1), axis=0).reshape(tok_rows, 2, width)
    first_weight = 1.0 / (1.0 + jnp.exp(route_logits[:, 1] - route_logits[:, 0]))
    second_weight = 1.0 / (1.0 + jnp.exp(route_logits[:, 0] - route_logits[:, 1]))
    weights = jnp.stack([first_weight, second_weight], axis=1)
    combined = jnp.sum(weights[:, :, None] * selected, axis=1).astype(jnp.bfloat16)
    return (combined, migrated[0], migrated[1], migrated[2])


def solution(mesh):
    placed = (
        P(("groups", "expert"), None),
        P(("groups", "expert"), None),
        P(("groups", "expert"), None),
        P(),
        P(),
        P(("groups", "expert"), None, None),
        P(("groups", "expert"), None, None),
        P(("groups", "expert"), None, None),
    )
    return jax.shard_map(
        per_device,
        mesh=mesh,
        in_specs=placed,
        out_specs=(
            P(("groups", "expert"), None),
            P(("groups", "expert"), None, None),
            P(("groups", "expert"), None, None),
            P(("groups", "expert"), None, None),
        ),
        check_vma=False,
    )
```

profile of v0, /device:TPU:31, one launch (start us, length us, event | category | flops | bytes accessed | tf_op | source)
XLA Modules:
  0.0 373.2 jit_solution(848314406968828936)
XLA Ops:
  5.1 6.3 %all-to-all-start = ((bf16[16,6,6144]{2,1,0:T(8,128)(2,1)}), bf16[16,6,6144]{2,1,0:T(8,128)(2,1)}, u32[]{:S(2)}, u32[]{:S(2)}) async-start(bf16[16,6,6144]{2,1,0:T(8,128)(2,1)} %broadcast_select_fusion.3), calls=%async_computation | async-start | bytes 3145728 | tf_op jit(solution)/shard_map/all_to_all | solution.py:56
  11.4 4.5 %copy.102 = bf16[1,6144,128]{2,0,1:T(2,128)(2,1)S(1)} copy(bf16[1,6144,128]{2,1,0:T(8,128)(2,1)} %param.15) | data formatting | bytes 3145728 | tf_op args[5]
  16.5 34.4 %reduce.2 = bf16[6144,128]{1,0:T(8,128)(2,1)} reduce(bf16[6144,1,128]{2,1,0:T(2,128)(2,1)S(1)} %bitcast.65, bf16[]{:T(256)} %broadcast.317), dimensions={1}, to_apply=%bitcast.64.reduce_sub_computation | reduce | bytes 3145730
  50.9 4.4 %reshape.287 = bf16[16,2,24576]{2,1,0:T(2,128)(2,1)} reshape(bf16[6144,128]{1,0:T(8,128)(2,1)} %reduce.2) | data formatting | bytes 3145728
  55.3 6.0 %all-to-all-start.2 = ((bf16[16,2,24576]{2,1,0:T(2,128)(2,1)}), bf16[16,2,24576]{2,1,0:T(2,128)(2,1)}, u32[]{:S(2)}, u32[]{:S(2)}) async-start(bf16[16,2,24576]{2,1,0:T(2,128)(2,1)} %reshape.287), calls=%async_computation.2 | async-start | bytes 3145728 | tf_op jit(solution)/shard_map/all_to_all | solution.py:27
  61.3 4.5 %copy.101 = bf16[1,6144,128]{2,0,1:T(2,128)(2,1)S(1)} copy(bf16[1,6144,128]{2,1,0:T(8,128)(2,1)} %param.16) | data formatting | bytes 3145728 | tf_op args[6]
  65.9 34.4 %reduce.1 = bf16[6144,128]{1,0:T(8,128)(2,1)} reduce(bf16[6144,1,128]{2,1,0:T(2,128)(2,1)S(1)} %bitcast.70, bf16[]{:T(256)} %broadcast.317), dimensions={1}, to_apply=%bitcast.63.reduce_sub_computation | reduce | bytes 3145730
  100.3 4.4 %reshape.289 = bf16[16,2,24576]{2,1,0:T(2,128)(2,1)} reshape(bf16[6144,128]{1,0:T(8,128)(2,1)} %reduce.1) | data formatting | bytes 3145728
  104.7 6.0 %all-to-all-start.4 = ((bf16[16,2,24576]{2,1,0:T(2,128)(2,1)}), bf16[16,2,24576]{2,1,0:T(2,128)(2,1)}, u32[]{:S(2)}, u32[]{:S(2)}) async-start(bf16[16,2,24576]{2,1,0:T(2,128)(2,1)} %reshape.289), calls=%async_computation.4 | async-start | bytes 3145728 | tf_op jit(solution)/shard_map/all_to_all | solution.py:28
  110.7 4.5 %copy.100 = bf16[1,6144,128]{2,0,1:T(2,128)(2,1)S(1)} copy(bf16[1,6144,128]{2,1,0:T(8,128)(2,1)} %param.17) | data formatting | bytes 3145728 | tf_op args[7]
  115.3 34.4 %reduce = bf16[6144,128]{1,0:T(8,128)(2,1)} reduce(bf16[6144,1,128]{2,1,0:T(2,128)(2,1)S(1)} %bitcast.66, bf16[]{:T(256)} %broadcast.317), dimensions={1}, to_apply=%bitcast.62.reduce_sub_computation | reduce | bytes 3145730
  149.7 4.4 %reshape.291 = bf16[16,2,24576]{2,1,0:T(2,128)(2,1)} reshape(bf16[6144,128]{1,0:T(8,128)(2,1)} %reduce) | data formatting | bytes 3145728
  154.1 6.0 %all-to-all-start.6 = ((bf16[16,2,24576]{2,1,0:T(2,128)(2,1)}), bf16[16,2,24576]{2,1,0:T(2,128)(2,1)S(1)}, u32[]{:S(2)}, u32[]{:S(2)}) async-start(bf16[16,2,24576]{2,1,0:T(2,128)(2,1)} %reshape.291), calls=%async_computation.6 | async-start | bytes 3145728 | tf_op jit(solution)/shard_map/all_to_all | solution.py:29
  163.6 4.0 %convolution_convert_fusion = bf16[96,6144]{1,0:T(8,128)(2,1)} fusion(bf16[1,6144,128]{2,1,0:T(8,128)(2,1)} %param.17, bf16[96,6144]{1,0:T(8,128)(2,1)S(1)} %reshape.214, bf16[1,6144,128]{2,1,0:T(8,128)(2,1)} %param.16, f32[96,128]{1,0:T(8,128)S(1)} %fusion.3), kind=kOutput, calls=%fused_computation.7 | convolution fusion | flops 302653440 | bytes 5554176 | tf_op jit(solution)/shard_map/dot_general | solution.py:63
  170.0 25.3 %all-to-all-done.6 = bf16[16,2,24576]{2,1,0:T(2,128)(2,1)S(1)} async-done(((bf16[16,2,24576]{2,1,0:T(2,128)(2,1)}), bf16[16,2,24576]{2,1,0:T(2,128)(2,1)S(1)}, u32[]{:S(2)}, u32[]{:S(2)}) %all-to-all-start.6) | async-done | bytes 1572896 | tf_op jit(solution)/shard_map/all_to_all | solution.py:29
  196.4 5.7 %all-to-all-start.1 = ((bf16[16,6,6144]{2,1,0:T(8,128)(2,1)}), bf16[16,6,6144]{2,1,0:T(8,128)(2,1)}, u32[]{:S(2)}, u32[]{:S(2)}) async-start(bf16[16,6,6144]{2,1,0:T(8,128)(2,1)} %reshape.215), calls=%async_computation.1 | async-start | bytes 3145728 | tf_op jit(solution)/shard_map/all_to_all | solution.py:67
  203.0 8.1 %reshape.288 = bf16[6144,1,128]{2,1,0:T(2,128)(2,1)S(1)} reshape(bf16[16,2,24576]{2,1,0:T(2,128)(2,1)} %all-to-all-done.2) | data formatting | bytes 3145728
  212.5 8.1 %reshape.290 = bf16[6144,1,128]{2,1,0:T(2,128)(2,1)S(1)} reshape(bf16[16,2,24576]{2,1,0:T(2,128)(2,1)} %all-to-all-done.4) | data formatting | bytes 3145728
  227.2 8.1 %reshape.292 = bf16[6144,1,128]{2,1,0:T(2,128)(2,1)S(1)} reshape(bf16[16,2,24576]{2,1,0:T(2,128)(2,1)} %copy-done.7) | data formatting | bytes 3145728
  240.1 3.8 %broadcast_select_fusion = (bf16[16,384,128]{2,1,0:T(8,128)(2,1)}, bf16[16,384,128]{2,1,0:T(8,128)(2,1)}, bf16[16,384,128]{2,1,0:T(8,128)(2,1)}) fusion(bf16[16,384,128]{2,1,0:T(8,128)(2,1)} %gather_fusion.6, pred[16]{0:T(512)(128)(4,1)S(1)} %get-tuple-element.5, bf16[16,384,128]{2,1,0:T(8,128)(2,1)S(1)} %copy-done.5, bf16[16,384,128]{2,1,0:T(8,128)(2,1)S(1)} %copy-done.4), kind=kLoop, calls=%fused_computation.14 | loop fusion | flops 2359296 | bytes 9437200 | tf_op jit(solution)/shard_map/jit(_take)/select_n | solution.py:34
  244.0 41.4 %all_to_all.82 = bf16[16,384,128]{2,1,0:T(8,128)(2,1)S(1)} all-to-all(bf16[16,384,128]{2,1,0:T(8,128)(2,1)} %get-tuple-element.17), channel_id=1, replica_groups=mesh['groups'=2,'expert'=16] {'expert'}, dimensions={0} | all-to-all | bytes 3145728 | tf_op jit(solution)/shard_map/all_to_all | solution.py:37
  285.4 40.9 %all_to_all.83 = bf16[16,384,128]{2,1,0:T(8,128)(2,1)} all-to-all(bf16[16,384,128]{2,1,0:T(8,128)(2,1)S(1)} %copy-done.6), channel_id=1, replica_groups=mesh['groups'=2,'expert'=16] {'expert'}, dimensions={0} | all-to-all | bytes 3145728 | tf_op jit(solution)/shard_map/all_to_all | solution.py:38
  326.2 5.9 %all-to-all-start.7 = ((bf16[16,384,128]{2,1,0:T(8,128)(2,1)}), bf16[16,384,128]{2,1,0:T(8,128)(2,1)}, u32[]{:S(2)}, u32[]{:S(2)}) async-start(bf16[16,384,128]{2,1,0:T(8,128)(2,1)} %get-tuple-element.15), calls=%async_computation.7 | async-start | bytes 3145728 | tf_op jit(solution)/shard_map/all_to_all | solution.py:39
  343.6 23.8 %all-to-all-done.7 = bf16[16,384,128]{2,1,0:T(8,128)(2,1)} async-done(((bf16[16,384,128]{2,1,0:T(8,128)(2,1)}), bf16[16,384,128]{2,1,0:T(8,128)(2,1)}, u32[]{:S(2)}, u32[]{:S(2)}) %all-to-all-start.7) | async-done | bytes 1572896 | tf_op jit(solution)/shard_map/all_to_all | solution.py:39
  (88 shorter events, 42.9 us)
Async XLA Ops:
  0.6 1.9 copy-start
  5.1 50.2 %all-to-all-start = ((bf16[16,6,6144]{2,1,0:T(8,128)(2,1)}), bf16[16,6,6144]{2,1,0:T(8,128)(2,1)}, u32[]{:S(2)}, u32[]{:S(2)}) async-start(bf16[16,6,6144]{2,1,0:T(8,128)(2,1)} %broadcast_select_fusion.3), calls=%async_computation | async-start | bytes 3145728 | tf_op jit(solution)/shard_map/all_to_all | solution.py:56
  55.3 49.4 %all-to-all-start.2 = ((bf16[16,2,24576]{2,1,0:T(2,128)(2,1)}), bf16[16,2,24576]{2,1,0:T(2,128)(2,1)}, u32[]{:S(2)}, u32[]{:S(2)}) async-start(bf16[16,2,24576]{2,1,0:T(2,128)(2,1)} %reshape.287), calls=%async_computation.2 | async-start | bytes 3145728 | tf_op jit(solution)/shard_map/all_to_all | solution.py:27
  104.7 49.4 %all-to-all-start.4 = ((bf16[16,2,24576]{2,1,0:T(2,128)(2,1)}), bf16[16,2,24576]{2,1,0:T(2,128)(2,1)}, u32[]{:S(2)}, u32[]{:S(2)}) async-start(bf16[16,2,24576]{2,1,0:T(2,128)(2,1)} %reshape.289), calls=%async_computation.4 | async-start | bytes 3145728 | tf_op jit(solution)/shard_map/all_to_all | solution.py:28
  154.1 41.2 %all-to-all-start.6 = ((bf16[16,2,24576]{2,1,0:T(2,128)(2,1)}), bf16[16,2,24576]{2,1,0:T(2,128)(2,1)S(1)}, u32[]{:S(2)}, u32[]{:S(2)}) async-start(bf16[16,2,24576]{2,1,0:T(2,128)(2,1)} %reshape.291), calls=%async_computation.6 | async-start | bytes 3145728 | tf_op jit(solution)/shard_map/all_to_all | solution.py:29
  170.0 32.2 %copy-start.11 = (s32[16]{0:T(128)S(1)}, s32[16]{0:T(128)}, u32[]{:S(2)}) copy-start(s32[16]{0:T(128)} %param.14) | copy-start | bytes 196
  170.0 32.3 %copy-start.2 = (s32[16]{0:T(128)S(1)}, s32[16]{0:T(128)}, u32[]{:S(2)}) copy-start(s32[16]{0:T(128)} %param.13) | copy-start | bytes 196
  195.3 1.1 copy-start.7
  196.4 47.5 %all-to-all-start.1 = ((bf16[16,6,6144]{2,1,0:T(8,128)(2,1)}), bf16[16,6,6144]{2,1,0:T(8,128)(2,1)}, u32[]{:S(2)}, u32[]{:S(2)}) async-start(bf16[16,6,6144]{2,1,0:T(8,128)(2,1)} %reshape.215), calls=%async_computation.1 | async-start | bytes 3145728 | tf_op jit(solution)/shard_map/all_to_all | solution.py:67
  221.9 3.4 copy-start.8
  236.7 3.5 copy-start.4
  236.7 3.5 copy-start.5
  244.0 41.4 %copy-start.6 = (bf16[16,384,128]{2,1,0:T(8,128)(2,1)S(1)}, bf16[16,384,128]{2,1,0:T(8,128)(2,1)}, u32[]{:S(2)}) copy-start(bf16[16,384,128]{2,1,0:T(8,128)(2,1)} %get-tuple-element.16) | copy-start | bytes 4718596
  326.2 5.9 %copy-start.9 = (s32[16,2]{0,1:T(2,128)S(1)}, s32[16,2]{0,1:T(2,128)}, u32[]{:S(2)}) copy-start(s32[16,2]{0,1:T(2,128)} %param.11) | copy-start | bytes 388
  326.2 41.2 %all-to-all-start.7 = ((bf16[16,384,128]{2,1,0:T(8,128)(2,1)}), bf16[16,384,128]{2,1,0:T(8,128)(2,1)}, u32[]{:S(2)}, u32[]{:S(2)}) async-start(bf16[16,384,128]{2,1,0:T(8,128)(2,1)} %get-tuple-element.15), calls=%async_computation.7 | async-start | bytes 3145728 | tf_op jit(solution)/shard_map/all_to_all | solution.py:39
  332.3 1.2 copy-start.10
  367.4 2.0 copy-start.3
  369.4 3.8 %copy-start.1 = (bf16[16,6144]{1,0:T(8,128)(2,1)S(1)}, bf16[16,6144]{1,0:T(8,128)(2,1)}, u32[]{:S(2)}) copy-start(bf16[16,6144]{1,0:T(8,128)(2,1)} %param.10) | copy-start | bytes 589828
where the time goes:
time: 377 us; the launch traced here: 373 us
  other arithmetic  112 us (30%)
  local copies, waits for them, and re-layouts  85.4 us (23%)
  blocking collectives  82.3 us (22%)
  waiting for transfers between devices  49.1 us (13%)
  starting transfers between devices  36 us (10%)
  matrix products  7.57 us (2%)
    unnamed x3, other arithmetic  103 us
    unnamed x41, local copies, waits for them, and re-layouts  64.7 us
    all_to_all x1, blocking collectives, per_device(): lax.all_to_all(reordered[0], 'expert', split_axis=0, concat_axis=1, tiled...  41.4 us
    all_to_all x1, blocking collectives, per_device(): lax.all_to_all(reordered[1], 'expert', split_axis=0, concat_axis=1, tiled...  40.9 us
    all_to_all x1, waiting for transfers between devices, per_device(): lax.all_to_all(held_down, 'expert', split_axis=1, concat_axis=0, tiled=True)  25.3 us
    all_to_all x1, waiting for transfers between devices, per_device(): lax.all_to_all(reordered[2], 'expert', split_axis=0, concat_axis=1, tiled...  23.8 us
  transfers between devices with their start and end apart: 6, of which 2 were waited for; matrix products, arithmetic and copies ran while one was open for 52% of the time, Pallas kernels for 0%

commit v1 on v0

v1 whole, which is shorter than its diff:
```python
import functools

import jax
import jax.numpy as jnp
from jax import lax
from jax.experimental import pallas as pl
from jax.experimental.pallas import tpu as pltpu
from jax.sharding import PartitionSpec as P

EXPERTS = 8
LANES = 128
MESH = pl.DeviceIdType.MESH
VMEM_BYTES = 63_000_000


def layer_kernel(
    n,
    source_of,
    tok,
    coef,
    held_g,
    held_u,
    held_d,
    out,
    moved_g,
    moved_u,
    moved_d,
    tok_all,
    coef_all,
    w_gu,
    w_d,
    pieces_g,
    pieces_u,
    pieces_d,
    ordered,
    hidden,
    contrib,
    arrived,
    cross_out,
    cross_in,
    load_sem,
    tok_send,
    tok_recv,
    fwd_send,
    one_send,
    one_recv,
    two_send,
    two_recv,
    part_send,
    part_recv,
    cross_send,
    cross_recv,
):
    me = lax.axis_index("expert")
    half = n // 2
    base = (me // half) * half
    lane = me - base
    twin = lax.rem(me + half, n)
    twin_base = lax.rem(base + half, n)
    rows, width = tok.shape
    band = width // n
    held = (held_g, held_u, held_d)
    moved = (moved_g, moved_u, moved_d)
    pieces = (pieces_g, pieces_u, pieces_d)

    barrier = pltpu.get_barrier_semaphore()

    @pl.loop(1, n)
    def _(k):
        pl.semaphore_signal(
            barrier, inc=1, device_id={"expert": lax.rem(me + k, n)}, device_id_type=MESH
        )

    loads = (
        pltpu.make_async_copy(held_g.at[0], w_gu.at[:, pl.ds(0, LANES)], load_sem.at[0]),
        pltpu.make_async_copy(held_u.at[0], w_gu.at[:, pl.ds(LANES, LANES)], load_sem.at[1]),
        pltpu.make_async_copy(held_d.at[0], w_d, load_sem.at[2]),
    )
    for load in loads:
        load.start()

    def token_rows(owner):
        return pl.ds(pl.multiple_of(owner * rows, rows), rows)

    def band_rows(owner):
        return pl.ds(pl.multiple_of(owner * band, band), band)

    tok_all[token_rows(me), :] = tok[...]
    coef_all[token_rows(me), :] = coef[...]
    pl.semaphore_wait(barrier, n - 1)

    def token_copy(peer):
        return (
            pltpu.make_async_remote_copy(
                src_ref=tok, dst_ref=tok_all.at[token_rows(me)],
                send_sem=tok_send.at[0, peer], recv_sem=tok_recv.at[0, me],
                device_id={"expert": peer}, device_id_type=MESH,
            ),
            pltpu.make_async_remote_copy(
                src_ref=coef, dst_ref=coef_all.at[token_rows(me)],
                send_sem=tok_send.at[1, peer], recv_sem=tok_recv.at[1, me],
                device_id={"expert": peer}, device_id_type=MESH,
            ),
        )

    def twin_copy(peer):
        return (
            pltpu.make_async_remote_copy(
                src_ref=tok_all.at[token_rows(twin)], dst_ref=tok_all.at[token_rows(twin)],
                send_sem=fwd_send.at[0, peer], recv_sem=tok_recv.at[0, twin],
                device_id={"expert": peer}, device_id_type=MESH,
            ),
            pltpu.make_async_remote_copy(
                src_ref=coef_all.at[token_rows(twin)], dst_ref=coef_all.at[token_rows(twin)],
                send_sem=fwd_send.at[1, peer], recv_sem=tok_recv.at[1, twin],
                device_id={"expert": peer}, device_id_type=MESH,
            ),
        )

    def tokens_arrive(owner):
        pltpu.make_async_copy(tok, tok_all.at[token_rows(owner)], tok_recv.at[0, owner]).wait()
        pltpu.make_async_copy(coef, coef_all.at[token_rows(owner)], tok_recv.at[1, owner]).wait()

    def near(k):
        return base + lax.rem(lane + k, half)

    def band_copy(array, peer):
        return pltpu.make_async_remote_copy(
            src_ref=held[array].at[0, band_rows(peer)], dst_ref=pieces[array].at[me],
            send_sem=one_send.at[array], recv_sem=one_recv.at[array],
            device_id={"expert": peer}, device_id_type=MESH,
        )

    def spread(array):
        pltpu.make_async_copy(
            held[array].at[0, band_rows(me)], pieces[array].at[me], one_recv.at[array]
        ).start()

        @pl.loop(1, n)
        def _(k):
            band_copy(array, lax.rem(me + k, n)).start()

    def deliver(array):
        pltpu.make_async_copy(pieces[array], pieces[array], one_recv.at[array]).wait()

        @pl.loop(0, n)
        def _(slot):
            ordered[array, slot] = pieces[array][source_of[slot]]

        pltpu.make_async_copy(
            ordered.at[array, me], moved[array].at[0, band_rows(me)], two_recv.at[array]
        ).start()

        @pl.loop(1, n)
        def _(k):
            peer = lax.rem(me + k, n)
            pltpu.make_async_remote_copy(
                src_ref=ordered.at[array, peer], dst_ref=moved[array].at[0, band_rows(me)],
                send_sem=two_send.at[array], recv_sem=two_recv.at[array],
                device_id={"expert": peer}, device_id_type=MESH,
            ).start()

    for copy in token_copy(twin):
        copy.start()

    @pl.loop(1, half)
    def _(k):
        for copy in token_copy(near(k)):
            copy.start()

    spread(0)
    tokens_arrive(twin)

    @pl.loop(1, half)
    def _(k):
        for copy in twin_copy(near(k)):
            copy.start()

    spread(1)
    spread(2)

    @pl.loop(1, half)
    def _(k):
        tokens_arrive(near(k))
        tokens_arrive(twin_base + lax.rem(lane + k, half))

    for load in loads:
        load.wait()

    step = min(256, n * rows)
    columns = 512

    @pl.loop(0, n * rows // step)
    def _(block):
        at = pl.ds(pl.multiple_of(block * step, step), step)
        both = jnp.dot(tok_all[at, :], w_gu[...], preferred_element_type=jnp.float32)
        gate_value = both[:, :LANES]
        up_value = both[:, LANES:]
        hidden[...] = (gate_value / (1.0 + jnp.exp(-gate_value)) * up_value).astype(jnp.bfloat16)
        lanes = lax.broadcasted_iota(jnp.int32, (step, LANES), 1)
        scale = jnp.sum(jnp.where(lanes == me, coef_all[at, :], 0.0), axis=1, keepdims=True)

        @pl.loop(0, width // columns)
        def _(part):
            cols = pl.ds(pl.multiple_of(part * columns, columns), columns)
            value = lax.dot_general(
                hidden[...], w_d[cols, :], (((1,), (1,)), ((), ())),
                preferred_element_type=jnp.float32,
            )
            value = value.astype(jnp.bfloat16).astype(jnp.float32)
            contrib[at, cols] = (value * scale).astype(jnp.bfloat16)

    def part_copy(kind, peer):
        owner = peer if kind == 0 else lax.rem(peer + half, n)
        return pltpu.make_async_remote_copy(
            src_ref=contrib.at[token_rows(owner)], dst_ref=arrived.at[kind, lane],
            send_sem=part_send.at[kind, peer - base], recv_sem=part_recv.at[kind, lane],
            device_id={"expert": peer}, device_id_type=MESH,
        )

    for kind in (1, 0):

        @pl.loop(1, half)
        def _(k):
            part_copy(kind, near(k)).start()

    def add_up(kind, owner, extra, target):
        @pl.loop(1, half)
        def _(k):
            other = lax.rem(lane + k, half)
            pltpu.make_async_copy(
                arrived.at[kind, other], arrived.at[kind, other], part_recv.at[kind, other]
            ).wait()

        @pl.loop(0, width // columns)
        def _(part):
            cols = pl.ds(pl.multiple_of(part * columns, columns), columns)

            def more(k, total):
                return total + arrived[kind, lax.rem(lane + k, half), :, cols].astype(jnp.float32)

            total = contrib[token_rows(owner), cols].astype(jnp.float32)
            if extra is not None:
                total = total + extra[:, cols].astype(jnp.float32)
            target[:, cols] = lax.fori_loop(1, half, more, total).astype(jnp.bfloat16)

    deliver(0)
    add_up(1, twin, None, cross_out)
    cross = pltpu.make_async_remote_copy(
        src_ref=cross_out, dst_ref=cross_in, send_sem=cross_send, recv_sem=cross_recv,
        device_id={"expert": twin}, device_id_type=MESH,
    )
    cross.start()
    deliver(1)
    deliver(2)
    cross.wait()
    add_up(0, me, cross_in, out)

    for copy in token_copy(twin):
        copy.wait_send()

    @pl.loop(1, half)
    def _(k):
        for copy in token_copy(near(k)):
            copy.wait_send()
        for copy in twin_copy(near(k)):
            copy.wait_send()
        part_copy(0, near(k)).wait_send()
        part_copy(1, near(k)).wait_send()

    for array in range(3):
        most = pieces[array].at[pl.ds(0, n - 1)]
        pltpu.make_async_copy(most, most, one_send.at[array]).wait()
        pltpu.make_async_copy(most, most, two_send.at[array]).wait()
        pltpu.make_async_copy(
            moved[array].at[0], moved[array].at[0], two_recv.at[array]
        ).wait()


def per_device(
    tokens, route_ids, route_logits, old_place, new_place, held_gate, held_up, held_down
):
    n = lax.axis_size("expert")
    rows, width = tokens.shape
    band = width // n
    half = n // 2
    device_ids = jnp.arange(n, dtype=jnp.int32)
    blocks = n // EXPERTS
    at_new = (new_place[:, None] == device_ids[None, :]).astype(jnp.int32)
    at_old = (old_place[:, None] == device_ids[None, :]).astype(jnp.int32)
    source_of = jnp.sum(at_new * old_place[:, None], axis=0)
    expert_at = jnp.sum(at_old * device_ids[:, None], axis=0) // blocks
    first_weight = 1.0 / (1.0 + jnp.exp(route_logits[:, 1] - route_logits[:, 0]))
    second_weight = 1.0 / (1.0 + jnp.exp(route_logits[:, 0] - route_logits[:, 1]))
    coef = jnp.where(route_ids[:, 0:1] == expert_at[None, :], first_weight[:, None], 0.0)
    coef = coef + jnp.where(route_ids[:, 1:2] == expert_at[None, :], second_weight[:, None], 0.0)
    coef = jnp.pad(coef, ((0, 0), (0, LANES - n)))

    vmem = pl.BlockSpec(memory_space=pltpu.VMEM)
    anywhere = pl.BlockSpec(memory_space=pl.ANY)
    dma = pltpu.SemaphoreType.DMA
    moved_shape = jax.ShapeDtypeStruct(held_gate.shape, held_gate.dtype)
    return pl.pallas_call(
        functools.partial(layer_kernel, n),
        out_shape=(
            jax.ShapeDtypeStruct((rows, width), jnp.bfloat16),
            moved_shape,
            moved_shape,
            moved_shape,
        ),
        in_specs=[pl.BlockSpec(memory_space=pltpu.SMEM), vmem, vmem] + [anywhere] * 3,
        out_specs=(vmem, anywhere, anywhere, anywhere),
        scratch_shapes=[
            pltpu.VMEM((n * rows, width), jnp.bfloat16),
            pltpu.VMEM((n * rows, LANES), jnp.float32),
            pltpu.VMEM((width, 2 * LANES), jnp.bfloat16),
            pltpu.VMEM((width, LANES), jnp.bfloat16),
            pltpu.VMEM((n, band, LANES), jnp.bfloat16),
            pltpu.VMEM((n, band, LANES), jnp.bfloat16),
            pltpu.VMEM((n, band, LANES), jnp.bfloat16),
            pltpu.VMEM((3, n, band, LANES), jnp.bfloat16),
            pltpu.VMEM((min(256, n * rows), LANES), jnp.bfloat16),
            pltpu.VMEM((n * rows, width), jnp.bfloat16),
            pltpu.VMEM((2, half, rows, width), jnp.bfloat16),
            pltpu.VMEM((rows, width), jnp.bfloat16),
            pltpu.VMEM((rows, width), jnp.bfloat16),
            dma((3,)),
            dma((2, n)),
            dma((2, n)),
            dma((2, n)),
            dma((3,)),
            dma((3,)),
            dma((3,)),
            dma((3,)),
            dma((2, half)),
            dma((2, half)),
            dma,
            dma,
        ],
        compiler_params=pltpu.CompilerParams(
            collective_id=0, has_side_effects=True, vmem_limit_bytes=VMEM_BYTES
        ),
    )(source_of, tokens, coef, held_gate, held_up, held_down)


def solution(mesh):
    split = ("groups", "expert")
    placed = (
        P(split, None),
        P(split, None),
        P(split, None),
        P(),
        P(),
        P(split, None, None),
        P(split, None, None),
        P(split, None, None),
    )
    return jax.shard_map(
        per_device,
        mesh=mesh,
        in_specs=placed,
        out_specs=(
            P(split, None),
            P(split, None, None),
            P(split, None, None),
            P(split, None, None),
        ),
        check_vma=False,
    )
```

time: 377 us -> 269 us (0.71); the launches traced: 373 us -> 269 us
  Pallas kernels: 0 us -> 258 us
  other arithmetic: 112 us -> 2.12 us
  blocking collectives: 82.3 us -> 0 us
  local copies, waits for them, and re-layouts: 85.4 us -> 8.87 us
  waiting for transfers between devices: 49.1 us -> 0 us
  starting transfers between devices: 36 us -> 0 us
  matrix products: 7.57 us -> 0 us
    pallas_call x0 -> x1, Pallas kernels: none -> 258 us  [per_device(): pl.pallas_call(functools.partial(layer_kernel, n), out_shape=(jax.ShapeDt...]
    unnamed x3 -> x0, other arithmetic: 103 us -> none
    all_to_all x2 -> x0, blocking collectives: 82.3 us -> none  [the longest x1 41.4 us: per_device(): lax.all_to_all(reordered[0], 'expert', split_axis=0, concat_axis=1, tiled...]
    unnamed x41 -> x8, local copies, waits for them, and re-layouts: 64.7 us -> 7.51 us
    all_to_all x6 -> x0, waiting for transfers between devices: 49.1 us -> none  [the longest x1 25.3 us: per_device(): lax.all_to_all(held_down, 'expert', split_axis=1, concat_axis=0, tiled=True)]
    all_to_all x6 -> x0, starting transfers between devices: 36 us -> none  [the longest x1 6.3 us: per_device(): lax.all_to_all(outgoing, 'expert', split_axis=0, concat_axis=0, tiled=True)]
    gather x12 -> x0, local copies, waits for them, and re-layouts: 14.4 us -> none  [the longest x1 3.45 us: per_device(): jnp.take(pieces[2], source_of, axis=0)]
    dot_general x4 -> x0, matrix products: 7.57 us -> none  [the longest x1 4 us: per_device(): lax.dot_general(hidden, w_down[0], (((1,), (1,)), ((), ())), preferred_el...]
  transfers between devices with their start and end apart: 6 -> 0, of which waited for: 2 -> 0; matrix products, arithmetic and copies ran while one was open for 52% -> 0% of each run, Pallas kernels for 0% -> 0%
where the time goes in v1:
time: 269 us
  Pallas kernels  258 us (96%)
  local copies, waits for them, and re-layouts  8.87 us (3%)
    pallas_call x1, Pallas kernels, per_device(): pl.pallas_call(functools.partial(layer_kernel, n), out_shape=(jax.ShapeDt...  258 us
    unnamed x8, local copies, waits for them, and re-layouts  7.51 us

profile of v1, /device:TPU:31, one launch (start us, length us, event | category | flops | bytes accessed | tf_op | source)
XLA Modules:
  0.0 269.3 jit_solution(15493523758901874775)
XLA Ops:
  0.6 0.8 slice_bitcast_fusion.1
  1.4 0.8 divide_bitcast_fusion.1
  2.2 1.3 select_reduce_fusion
  3.4 0.1 select_add_fusion
  3.5 0.6 pad.4.coef
  4.1 257.6 %shard_map.111 = (bf16[16,6144]{1,0:T(8,128)(2,1)}, bf16[1,6144,128]{2,1,0:T(8,128)(2,1)}, bf16[1,6144,128]{2,1,0:T(8,128)(2,1)}, bf16[1,6144,128]{2,1,0:T(8,128)(2,1)}) custom-call(s32[16]{0:T(128)} %get-tuple-element.5.source_of, bf16[16,6144]{1,0:T(8,128)(2,1)} %tok.1, f32[16,128]{1,0:T(8,128)} %pad.4.coef, bf16[1,6144,128]{2,1,0:T(8,128)(2,1)} %held_g.1, ...), custom_call_target="tpu_custom_call" | custom-call | tf_op jit(solution)/shard_map/pallas_call | solution.py:303
  261.7 1.6 copy.16
  263.4 0.0 copy-start.1
  263.4 2.8 %copy.17 = bf16[1,6144,128]{2,1,0:T(8,128)(2,1)} copy(bf16[1,6144,128]{2,1,0:T(8,128)(2,1)} %get-tuple-element.15) | data formatting | bytes 3145728
  266.1 0.0 copy-done.1
  266.1 0.0 copy-start
  266.1 1.1 copy.18
  267.3 0.8 copy-done
  268.1 1.1 copy.19
  (1 shorter events, 0.0 us)
Async XLA Ops:
  263.4 2.8 %copy-start.1 = (bf16[1,6144,128]{2,1,0:T(8,128)(2,1)S(1)}, bf16[1,6144,128]{2,1,0:T(8,128)(2,1)}, u32[]{:S(2)}) copy-start(bf16[1,6144,128]{2,1,0:T(8,128)(2,1)} %get-tuple-element.16) | copy-start | bytes 4718596
  266.1 2.0 copy-start
